TPU v7x, 32 devices: a whole 2x2x4 slice. The times are simulated.
32 devices in a mesh: band: 8 (over z, x), sub: 4 (over y, core).
Axes of the slice: x: 2, y: 2, z: 4, core: 2. Of those that a mesh axis runs over, the one named last changes fastest.
Arguments:
- grad_pred: bfloat16 [227, 24576], P(None, ('band', 'sub')), may hold values from -6 to 6
- grid_latent: bfloat16 [24576, 512], P(('band', 'sub')), may hold values from -6 to 6
- mesh_latent: bfloat16 [10240, 512], P(('band', 'sub')), may hold values from -6 to 6
- send_slot: int32 [24576], P(('band', 'sub')), may hold values from 0 to 2303, as said below
- edge_src: int32 [3, 73728], P(None, ('band', 'sub')), may hold values from 0 to 10239, as said below
- w_mesh: bfloat16 [512, 512], replicated, may hold values from -0.25 to 0.25
- w_grid: bfloat16 [512, 512], replicated, may hold values from -0.25 to 0.25
- w_msg: bfloat16 [512, 512], replicated, may hold values from -0.25 to 0.25
- w_out: bfloat16 [512, 227], replicated, may hold values from -0.25 to 0.25
Outputs:
- mesh_grad: bfloat16 [10240, 512], P(('band', 'sub'))
- grad_w_mesh: float32 [512, 512], replicated
- grad_w_grid: float32 [512, 512], replicated
- grad_w_msg: float32 [512, 512], replicated
- grad_w_out: float32 [512, 227], replicated
Inputs may be any that keep to these rules, and one draw needn't show every extreme that they name: For grid point p on latitude-major device i, send_slot[p] = j * 72 + r names patch-major device j and a rank r. On one device i the values are distinct, and for each j the ranks used are 0 to the count of i's points sent to j minus 1. Every such count is at most 72, and 72 is reached in every draw. Every grid point thereby gets one patch-major slot; live slots of each source stand at the front of its block of 72. One patch-major device holds at most 1920 live slots, reached on some device in every draw. `edge_src`: A slot on patch-major device j, of band b = j // 4, names senders in patch b only: mesh rows b * 1280 to (b + 1) * 1280 - 1. Entries of empty slots lie in that range too and are not read.
All inputs are finite; a program needn't handle non-finite values.
Results may differ from a plain program's by a relative error of at most 0.0076.
Values may be sent and summed in bfloat16 or wider, within the bound.
No kernel may reach another device: no remote copies, remote signals or barrier semaphores. Data moves between devices by JAX's collectives and lax.ppermute only.
A program may use at most 128 MiB of HBM per device.

v0:
```python
import math
import jax
import jax.numpy as jnp
from jax import lax
from jax.sharding import PartitionSpec as P


def latitude_weight(points, total):
    angle = jnp.pi * ((points.astype(jnp.float32) + 0.5) / total - 0.5)
    return 0.5 * jnp.pi * jnp.cos(angle)


def silu_slope(value):
    sigma = jax.nn.sigmoid(value)
    return sigma * (1.0 + value * (1.0 - sigma))


def contract_rows(left, right):
    return lax.dot_general(
        left, right, (((0,), (0,)), ((), ())), preferred_element_type=jnp.float32
    )


def times_transpose(left, right):
    return lax.dot_general(
        left, right, (((1,), (1,)), ((), ())), preferred_element_type=jnp.float32
    )


def shards(grad_pred, grid_latent, mesh_latent, send_slot, edge_src, w_mesh, w_grid, w_msg, w_out):
    grid_rows = grid_latent.shape[0]
    width = grid_latent.shape[1]
    channels = grad_pred.shape[0]
    devices = lax.axis_size(("band", "sub"))
    capacity = 3 * grid_rows // devices
    total_points = grid_rows * devices
    own_index = lax.axis_index(("band", "sub"))
    points = own_index * grid_rows + jnp.arange(grid_rows, dtype=jnp.int32)
    weighted = (
        latitude_weight(points, total_points)[None, :] * grad_pred.astype(jnp.float32)
    ).astype(jnp.bfloat16)
    target = send_slot // capacity
    slot_rank = send_slot % capacity
    joined = jnp.concatenate([grid_latent, weighted.T], axis=1)
    row_width = width + channels
    send_buffer = (
        jnp.zeros((devices, capacity, row_width), jnp.bfloat16).at[target, slot_rank].set(joined)
    )
    received = lax.all_to_all(send_buffer, ("band", "sub"), split_axis=0, concat_axis=0, tiled=True)
    slots = devices * capacity
    slot_rows = received.reshape(slots, row_width)
    latent_rows = slot_rows[:, :width]
    grad_rows = slot_rows[:, width:]
    grid_proj = jnp.dot(latent_rows, w_grid, preferred_element_type=jnp.float32).astype(
        jnp.bfloat16
    )
    mesh_proj = jnp.dot(mesh_latent, w_mesh, preferred_element_type=jnp.float32).astype(
        jnp.bfloat16
    )
    patch_proj = lax.all_gather(mesh_proj, "sub", axis=0, tiled=True)
    patch_size = patch_proj.shape[0]
    band_index = lax.axis_index("band")
    local_node = edge_src - band_index * patch_size
    grid_float = grid_proj.astype(jnp.float32)
    pre_acts = [
        patch_proj[local_node[corner]].astype(jnp.float32) + grid_float for corner in range(3)
    ]
    act_sum = (
        jax.nn.silu(pre_acts[0]) + jax.nn.silu(pre_acts[1]) + jax.nn.silu(pre_acts[2])
    ).astype(jnp.bfloat16)
    aggregate = jnp.dot(act_sum, w_msg, preferred_element_type=jnp.float32).astype(jnp.bfloat16)
    out_part = contract_rows(aggregate, grad_rows)
    agg_rows = times_transpose(grad_rows, w_out).astype(jnp.bfloat16)
    msg_part = contract_rows(act_sum, agg_rows)
    out_total = lax.psum(out_part, ("band", "sub"))
    msg_total = lax.psum(msg_part, ("band", "sub"))
    act_grad = times_transpose(agg_rows, w_msg)
    pre_grads = [(act_grad * silu_slope(pre)).astype(jnp.bfloat16) for pre in pre_acts]
    grid_proj_grad = (
        pre_grads[0].astype(jnp.float32)
        + pre_grads[1].astype(jnp.float32)
        + pre_grads[2].astype(jnp.float32)
    ).astype(jnp.bfloat16)
    node_part = jnp.zeros((patch_size, width), jnp.float32)
    for corner in range(3):
        node_part = node_part.at[local_node[corner]].add(pre_grads[corner].astype(jnp.float32))
    node_total = lax.psum_scatter(node_part, "sub", scatter_dimension=0, tiled=True)
    grid_part = contract_rows(latent_rows, grid_proj_grad)
    mesh_proj_grad = node_total.astype(jnp.bfloat16)
    mesh_grad = times_transpose(mesh_proj_grad, w_mesh).astype(jnp.bfloat16)
    mesh_part = contract_rows(mesh_latent, mesh_proj_grad)
    grad_scale = 1.0 / math.sqrt(3.0 * total_points)
    grid_total = lax.psum(grid_part, ("band", "sub"))
    mesh_total = lax.psum(mesh_part, ("band", "sub"))
    return (
        mesh_grad,
        mesh_total * grad_scale,
        grid_total * grad_scale,
        msg_total * grad_scale,
        out_total * grad_scale,
    )


def solution(mesh):
    placed = (
        P(None, ("band", "sub")),
        P(("band", "sub"), None),
        P(("band", "sub"), None),
        P(("band", "sub")),
        P(None, ("band", "sub")),
        P(),
        P(),
        P(),
        P(),
    )
    return jax.shard_map(
        shards,
        mesh=mesh,
        in_specs=placed,
        out_specs=(P(("band", "sub"), None), P(), P(), P(), P()),
        check_vma=False,
    )
```

profile of v0, /device:TPU:0, one launch (start us, length us, event | category | flops | bytes accessed | tf_op | source)
XLA Modules:
  0.0 467.4 jit_solution(4389432427457058807)
XLA Ops:
  7.2 0.8 compare_select_fusion.4
  8.0 1.0 fusion.15
  9.2 1.2 pad_maximum_fusion
  10.5 2.0 broadcast_in_dim.9
  12.5 101.6 %scatter_fusion = bf16[32,72,739]{2,1,0:T(8,128)(2,1)} fusion(bf16[32,72,739]{2,1,0:T(8,128)(2,1)} %broadcast_in_dim.9, s32[768]{0:T(1024)S(1)} %fusion.23, bf16[768,739]{1,0:T(8,128)(2,1)S(1)} %pad_maximum_fusion), kind=kCustom, calls=%fused_computation.3 | custom fusion | bytes 3411456 | tf_op jit(solution)/shard_map/scatter | solution.py:47
  114.1 7.4 %all-to-all-start = ((bf16[32,72,739]{2,1,0:T(8,128)(2,1)}), bf16[32,72,739]{2,1,0:T(8,128)(2,1)}, u32[]{:S(2)}, u32[]{:S(2)}) async-start(bf16[32,72,739]{2,1,0:T(8,128)(2,1)} %scatter_fusion), calls=%async_computation | async-start | bytes 7077888 | tf_op jit(solution)/shard_map/all_to_all | solution.py:49
  121.6 1.1 convolution_convert_fusion.4
  122.9 33.9 %all-gather.2.cloned.1.call-done = bf16[1280,512]{1,0:T(8,128)(2,1)} async-done(((bf16[320,512]{1,0:T(8,128)(2,1)}), bf16[1280,512]{1,0:T(8,128)(2,1)}) %all-gather.2.cloned.1.call-update) | async-done | bytes 1310736 | tf_op jit(solution)/shard_map/all_gather | solution.py:60
  156.9 9.2 %gather_fusion.2 = bf16[2304,512]{1,0:T(8,128)(2,1)} fusion(bf16[1280,512]{1,0:T(8,128)(2,1)} %all-gather.2.cloned.1.call-done, s32[3072]{0:T(1024)S(1)} %get-tuple-element.33), kind=kCustom, calls=%fused_computation.2 | custom fusion | bytes 4727808 | tf_op jit(solution)/shard_map/gather | solution.py:66
  166.1 7.5 %gather_fusion.1 = bf16[2304,512]{1,0:T(8,128)(2,1)} fusion(bf16[1280,512]{1,0:T(8,128)(2,1)S(1)} %copy-done.1, s32[3072]{0:T(1024)S(1)} %get-tuple-element.34), kind=kCustom, calls=%fused_computation.1 | custom fusion | bytes 4727808 | tf_op jit(solution)/shard_map/gather | solution.py:66
  173.6 7.5 %gather_fusion = bf16[2304,512]{1,0:T(8,128)(2,1)} fusion(bf16[1280,512]{1,0:T(8,128)(2,1)S(1)} %copy-done.1, s32[3072]{0:T(1024)S(1)} %pad_clamp_fusion.2), kind=kCustom, calls=%fused_computation | custom fusion | bytes 4727808 | tf_op jit(solution)/shard_map/gather | solution.py:66
  181.1 20.5 %all-to-all-done = bf16[32,72,739]{2,1,0:T(8,128)(2,1)} async-done(((bf16[32,72,739]{2,1,0:T(8,128)(2,1)}), bf16[32,72,739]{2,1,0:T(8,128)(2,1)}, u32[]{:S(2)}, u32[]{:S(2)}) %all-to-all-start) | async-done | bytes 3405344 | tf_op jit(solution)/shard_map/all_to_all | solution.py:49
  201.6 2.0 convolution_convert_fusion.2
  203.7 3.9 convolution_convert_fusion.1
  208.4 9.1 %multiply_convert_fusion = (bf16[2304,512]{1,0:T(8,128)(2,1)}, bf16[2304,512]{1,0:T(8,128)(2,1)}, bf16[2304,512]{1,0:T(8,128)(2,1)}, bf16[2304,512]{1,0:T(8,128)(2,1)}) fusion(bf16[2304,512]{1,0:T(8,128)(2,1)S(1)} %convolution_convert_fusion.1, bf16[2304,512]{1,0:T(8,128)(2,1)S(1)} %copy-done.6, bf16[2304,512]{1,0:T(8,128)(2,1)S(1)} %copy-done.7, ...), kind=kOutput, calls=%fused_computation.20 | convolution fusion | flops 1255145472 | bytes 21757952 | tf_op jit(solution)/shard_map/dot_general | solution.py:25
  217.4 17.0 %scatter_custom_fusion.1 = f32[1280,512]{1,0:T(8,128)S(1)} fusion(s32[2304]{0:T(1024)S(1)} %get-tuple-element.22, bf16[2304,512]{1,0:T(8,128)(2,1)} %get-tuple-element.30, f32[]{:T(128)} %constant.20.clone.1), kind=kCustom, calls=%fused_computation.16 | custom fusion | flops 2359296 | bytes 4980740 | tf_op jit(solution)/shard_map/scatter-add | solution.py:86
  234.5 17.5 %scatter_custom_fusion.2 = f32[1280,512]{1,0:T(8,128)S(1)} fusion(f32[1280,512]{1,0:T(8,128)S(1)} %scatter_custom_fusion.1, s32[2304]{0:T(1024)S(1)} %get-tuple-element.21, bf16[2304,512]{1,0:T(8,128)(2,1)} %get-tuple-element.28), kind=kCustom, calls=%fused_computation.14 | custom fusion | flops 2359296 | bytes 4980736 | tf_op jit(solution)/shard_map/scatter-add | solution.py:86
  252.0 17.4 %scatter_custom_fusion.3 = f32[1280,512]{1,0:T(8,128)S(1)} fusion(f32[1280,512]{1,0:T(8,128)S(1)} %scatter_custom_fusion.2, s32[2304]{0:T(1024)S(1)} %get-tuple-element.20, bf16[2304,512]{1,0:T(8,128)(2,1)} %get-tuple-element.27), kind=kCustom, calls=%fused_computation.11 | custom fusion | flops 2359296 | bytes 4980736 | tf_op jit(solution)/shard_map/scatter-add | solution.py:86
  269.4 1.5 copy-done.2
  271.2 4.8 %fusion.24 = f32[512,512]{0,1:T(8,128)} fusion(bf16[2304,512]{1,0:T(8,128)(2,1)} %get-tuple-element.29, bf16[2304,512]{1,0:T(8,128)(2,1)} %copy-done.5), kind=kOutput, calls=%fused_computation.74 | convolution fusion | flops 1207959552 | bytes 5767168 | tf_op jit(solution)/shard_map/dot_general | solution.py:19
  275.9 5.0 %fusion.12 = f32[512,227]{0,1:T(8,128)} fusion(bf16[2304,739]{1,0:T(8,128)(2,1)} %bitcast.2, bf16[2304,512]{1,0:T(8,128)(2,1)} %get-tuple-element.29, bf16[512,512]{1,0:T(8,128)(2,1)S(1)} %copy-done), kind=kOutput, calls=%fused_computation.37 | convolution fusion | flops 1744699392 | bytes 4528128 | tf_op jit(solution)/shard_map/dot_general | solution.py:19
  280.9 5.5 %fusion.7 = f32[512,512]{0,1:T(8,128)} fusion(bf16[2304,512]{1,0:T(8,128)(2,1)} %get-tuple-element.27, bf16[2304,512]{1,0:T(8,128)(2,1)} %get-tuple-element.28, bf16[2304,512]{1,0:T(8,128)(2,1)S(1)} %copy-done.4, bf16[2304,739]{1,0:T(8,128)(2,1)} %bitcast.2), kind=kOutput, calls=%fused_computation.29 | convolution fusion | flops 1215037440 | bytes 10485760 | tf_op jit(solution)/shard_map/dot_general | solution.py:19
  286.5 19.3 %reduce-scatter.2.cloned.1.call-done = f32[320,512]{1,0:T(8,128)} async-done(((f32[1280,512]{1,0:T(8,128)}), f32[320,512]{1,0:T(8,128)}) %reduce-scatter.2.cloned.1.call-update) | async-done | bytes 655376 | tf_op jit(solution)/shard_map/reduce_scatter | solution.py:87
  305.8 2.6 convolution_bitcast_fusion
  308.4 1.1 convolution_convert_fusion.3
  309.5 143.8 %all-reduce.3.cloned.1.call-done = (f32[512,512]{0,1:T(8,128)}, f32[512,512]{0,1:T(8,128)}, f32[512,512]{0,1:T(8,128)}, f32[512,227]{0,1:T(8,128)}) async-done(((f32[512,512]{0,1:T(8,128)}, f32[512,512]{0,1:T(8,128)}, f32[512,512]{0,1:T(8,128)}, f32[512,227]{0,1:T(8,128)}), (f32[512,512]{0,1:T(8,128)}, f32[512,512]{0,1:T(8,128)}, f32[512,512]{0,1:T(8,128)}, ...) | async-done | bytes 3610640 | tf_op jit(solution)/shard_map/psum | solution.py:94
  453.3 1.4 broadcast_multiply_fusion.2
  454.7 1.3 copy.29
  456.0 0.8 broadcast_multiply_fusion.3
  456.8 1.3 broadcast_multiply_fusion.1
  458.2 1.3 copy.30
  459.6 1.3 copy.31
  (47 shorter events, 1.6 us)
Async XLA Ops:
  7.2 200.5 %copy-start = (bf16[512,512]{1,0:T(8,128)(2,1)S(1)}, bf16[512,512]{1,0:T(8,128)(2,1)}, u32[]{:S(2)}) copy-start(bf16[512,512]{1,0:T(8,128)(2,1)} %param.16) | copy-start | bytes 1572868
  114.1 7.5 %copy-start.9 = (bf16[512,512]{1,0:T(8,128)(2,1)S(1)}, bf16[512,512]{1,0:T(8,128)(2,1)}, u32[]{:S(2)}) copy-start(bf16[512,512]{1,0:T(8,128)(2,1)} %param.14) | copy-start | bytes 1572868
  114.1 7.5 %copy-start.11 = (bf16[320,512]{1,0:T(8,128)(2,1)S(1)}, bf16[320,512]{1,0:T(8,128)(2,1)}, u32[]{:S(2)}) copy-start(bf16[320,512]{1,0:T(8,128)(2,1)} %param.11) | copy-start | bytes 983044
  114.1 8.7 %copy-start.15 = (s32[3,2304]{1,0:T(4,128)S(1)}, s32[3,2304]{1,0:T(4,128)}, u32[]{:S(2)}) copy-start(s32[3,2304]{1,0:T(4,128)} %param.13) | copy-start | bytes 82948
  114.1 87.5 %all-to-all-start = ((bf16[32,72,739]{2,1,0:T(8,128)(2,1)}), bf16[32,72,739]{2,1,0:T(8,128)(2,1)}, u32[]{:S(2)}, u32[]{:S(2)}) async-start(bf16[32,72,739]{2,1,0:T(8,128)(2,1)} %scatter_fusion), calls=%async_computation | async-start | bytes 7077888 | tf_op jit(solution)/shard_map/all_to_all | solution.py:49
  121.6 35.3 %all-gather.2.cloned.1.call-start = ((), (), s32[]{:S(2)}) async-start(), calls=%async_computation.2 | async-start | bytes 1638400 | tf_op jit(solution)/shard_map/all_gather | solution.py:60
  122.7 183.0 %reduce-scatter.2.cloned.1.call-start = ((), (), s32[]{:S(2)}) async-start(), calls=%async_computation.3 | async-start | bytes 3276800 | tf_op jit(solution)/shard_map/reduce_scatter | solution.py:87
  156.9 9.2 %copy-start.1 = (bf16[1280,512]{1,0:T(8,128)(2,1)S(1)}, bf16[1280,512]{1,0:T(8,128)(2,1)}, u32[]{:S(2)}) copy-start(bf16[1280,512]{1,0:T(8,128)(2,1)} %all-gather.2.cloned.1.call-done) | copy-start | bytes 3932164
  173.6 28.0 %copy-start.14 = (bf16[512,227]{0,1:T(8,128)(2,1)S(1)}, bf16[512,227]{0,1:T(8,128)(2,1)}, u32[]{:S(2)}) copy-start(bf16[512,227]{0,1:T(8,128)(2,1)} %param.17) | copy-start | bytes 697348
  181.1 22.6 %copy-start.16 = (bf16[512,512]{1,0:T(8,128)(2,1)S(1)}, bf16[512,512]{1,0:T(8,128)(2,1)}, u32[]{:S(2)}) copy-start(bf16[512,512]{1,0:T(8,128)(2,1)} %param.15) | copy-start | bytes 1572868
  203.7 4.0 copy-start.5
  203.7 4.0 copy-start.6
  203.7 4.0 copy-start.7
  203.7 4.6 copy-start.8
  269.4 1.5 copy-start.2
  270.9 182.4 %all-reduce.3.cloned.1.call-start = ((), (), s32[]{:S(2)}) async-start(), calls=%async_computation.4 | async-start | bytes 7241728 | tf_op jit(solution)/shard_map/psum | solution.py:94
  275.9 5.0 %copy-start.4 = (bf16[2304,512]{1,0:T(8,128)(2,1)S(1)}, bf16[2304,512]{1,0:T(8,128)(2,1)}, u32[]{:S(2)}) copy-start(bf16[2304,512]{1,0:T(8,128)(2,1)} %get-tuple-element.30) | copy-start | bytes 7077892
  286.5 21.9 %copy-start.10 = (bf16[512,512]{1,0:T(8,128)(2,1)S(1)}, bf16[512,512]{1,0:T(8,128)(2,1)}, u32[]{:S(2)}) copy-start(bf16[512,512]{1,0:T(8,128)(2,1)} %param.14) | copy-start | bytes 1572868
  305.8 2.6 copy-start.3
  453.3 2.7 copy-start.13
  456.0 3.5 copy-start.12
Sparse Core Ops, SparseCore 0:
  124.5 32.3 all-gather.1
  271.0 34.7 reduce-scatter.1
  312.4 140.8 all-reduce.2
where the time goes:
time: 472 us; the launch traced here: 467 us
  waiting for transfers between devices  218 us (46%)
  local copies, waits for them, and re-layouts  134 us (28%)
  other arithmetic  58.8 us (12%)
  matrix products  35.1 us (7%)
  between operations  14 us (3%)
  starting transfers between devices  7.79 us (2%)
    psum x1, waiting for transfers between devices, shards(): mesh_total = lax.psum(mesh_part, ('band', 'sub'))  144 us
    scatter x1, local copies, waits for them, and re-layouts, shards(): jnp.zeros((devices, capacity, row_width), jnp.bfloat16)  102 us
    scatter-add x3, other arithmetic, shards(): node_part.at[local_node[corner]].add(pre_grads[corner].astype(jnp.float32))  51.9 us
    all_gather x1, waiting for transfers between devices, shards(): patch_proj = lax.all_gather(mesh_proj, 'sub', axis=0, tiled=True)  33.9 us
    gather x3, local copies, waits for them, and re-layouts, shards(): patch_proj[local_node[corner]].astype(jnp.float32) + grid_float  24.2 us
    all_to_all x1, waiting for transfers between devices, shards(): lax.all_to_all(send_buffer, ('band', 'sub'), split_axis=0, concat_axis=0,...  20.5 us
    reduce_scatter x1, waiting for transfers between devices, shards(): lax.psum_scatter(node_part, 'sub', scatter_dimension=0, tiled=True)  19.3 us
    dot_general x4, matrix products, contract_rows(): lax.dot_general(left, right, (((0,), (0,)), ((), ())), preferred_element_...  17.9 us
  transfers between devices with their start and end apart: 4, of which 4 were waited for; matrix products, arithmetic and copies ran while one was open for 9% of the time, Pallas kernels for 0%

commit v1 on v0

--- a/solution.py
+++ b/solution.py
@@ -91,7 +91,7 @@
     mesh_part = contract_rows(mesh_latent, mesh_proj_grad)
     grad_scale = 1.0 / math.sqrt(3.0 * total_points)
     grid_total = lax.psum(grid_part, ("band", "sub"))
-    mesh_total = lax.psum(mesh_part, ("band", "sub"))
+    mesh_total = jnp.sum(lax.all_gather(mesh_part, ("band", "sub")), axis=0)
     return (
         mesh_grad,
         mesh_total * grad_scale,

time: 472 us -> 701 us (1.49)
  waiting for transfers between devices: 218 us -> 409 us
  local copies, waits for them, and re-layouts: 134 us -> 163 us
  other arithmetic: 58.8 us -> 66.9 us
    all_gather x0 -> x1, waiting for transfers between devices: none -> 195 us  [shards(): mesh_total = jnp.sum(lax.all_gather(mesh_part, ('band', 'sub')), axis=0)]
    unnamed x37 -> x33, local copies, waits for them, and re-layouts: 6.12 us -> 34.7 us
  transfers between devices with their start and end apart: 4 -> 5, of which waited for: 4 -> 5; matrix products, arithmetic and copies ran while one was open for 9% -> 7% of each run, Pallas kernels for 0% -> 0%
where the time goes in v1:
time: 701 us; the launch traced here: 696 us
  waiting for transfers between devices  409 us (58%)
  local copies, waits for them, and re-layouts  163 us (23%)
  other arithmetic  66.9 us (10%)
  matrix products  35.2 us (5%)
  between operations  14 us (2%)
  starting transfers between devices  7.88 us (1%)
    all_gather x1, waiting for transfers between devices, shards(): mesh_total = jnp.sum(lax.all_gather(mesh_part, ('band', 'sub')), axis=0)  195 us
    psum x1, waiting for transfers between devices, shards(): grid_total = lax.psum(grid_part, ('band', 'sub'))  141 us
    scatter x1, local copies, waits for them, and re-layouts, shards(): jnp.zeros((devices, capacity, row_width), jnp.bfloat16)  101 us
    scatter-add x3, other arithmetic, shards(): node_part.at[local_node[corner]].add(pre_grads[corner].astype(jnp.float32))  51.9 us
    unnamed x33, local copies, waits for them, and re-layouts  34.7 us
    all_gather x1, waiting for transfers between devices, shards(): patch_proj = lax.all_gather(mesh_proj, 'sub', axis=0, tiled=True)  33.9 us
    gather x3, local copies, waits for them, and re-layouts, shards(): patch_proj[local_node[corner]].astype(jnp.float32) + grid_float  24.2 us
    all_to_all x1, waiting for transfers between devices, shards(): lax.all_to_all(send_buffer, ('band', 'sub'), split_axis=0, concat_axis=0,...  20.5 us
  transfers between devices with their start and end apart: 5, of which 5 were waited for; matrix products, arithmetic and copies ran while one was open for 7% of the time, Pallas kernels for 0%

profile of v1, /device:TPU:0, one launch (start us, length us, event | category | flops | bytes accessed | tf_op | source)
XLA Modules:
  0.0 696.4 jit_solution(13431130467066327387)
XLA Ops:
  8.0 1.0 fusion.15
  9.2 1.2 pad_maximum_fusion
  10.5 2.0 broadcast_in_dim.9
  12.5 101.4 %scatter_fusion = bf16[32,72,739]{2,1,0:T(8,128)(2,1)} fusion(bf16[32,72,739]{2,1,0:T(8,128)(2,1)} %broadcast_in_dim.9, s32[768]{0:T(1024)S(1)} %fusion.23, bf16[768,739]{1,0:T(8,128)(2,1)S(1)} %pad_maximum_fusion), kind=kCustom, calls=%fused_computation.3 | custom fusion | bytes 3411456 | tf_op jit(solution)/shard_map/scatter | solution.py:47
  114.0 7.5 %all-to-all-start = ((bf16[32,72,739]{2,1,0:T(8,128)(2,1)}), bf16[32,72,739]{2,1,0:T(8,128)(2,1)}, u32[]{:S(2)}, u32[]{:S(2)}) async-start(bf16[32,72,739]{2,1,0:T(8,128)(2,1)} %scatter_fusion), calls=%async_computation | async-start | bytes 7077888 | tf_op jit(solution)/shard_map/all_to_all | solution.py:49
  121.5 1.1 convolution_convert_fusion.4
  122.8 33.9 %all-gather.4.cloned.1.call-done = bf16[1280,512]{1,0:T(8,128)(2,1)} async-done(((bf16[320,512]{1,0:T(8,128)(2,1)}), bf16[1280,512]{1,0:T(8,128)(2,1)}) %all-gather.4.cloned.1.call-update) | async-done | bytes 1310736 | tf_op jit(solution)/shard_map/all_gather | solution.py:60
  156.8 9.2 %gather_fusion.2 = bf16[2304,512]{1,0:T(8,128)(2,1)} fusion(bf16[1280,512]{1,0:T(8,128)(2,1)} %all-gather.4.cloned.1.call-done, s32[3072]{0:T(1024)S(1)} %get-tuple-element.17), kind=kCustom, calls=%fused_computation.2 | custom fusion | bytes 4727808 | tf_op jit(solution)/shard_map/gather | solution.py:66
  166.0 7.5 %gather_fusion.1 = bf16[2304,512]{1,0:T(8,128)(2,1)} fusion(bf16[1280,512]{1,0:T(8,128)(2,1)S(1)} %copy-done.1, s32[3072]{0:T(1024)S(1)} %get-tuple-element.18), kind=kCustom, calls=%fused_computation.1 | custom fusion | bytes 4727808 | tf_op jit(solution)/shard_map/gather | solution.py:66
  173.5 7.5 %gather_fusion = bf16[2304,512]{1,0:T(8,128)(2,1)} fusion(bf16[1280,512]{1,0:T(8,128)(2,1)S(1)} %copy-done.1, s32[3072]{0:T(1024)S(1)} %pad_clamp_fusion.2), kind=kCustom, calls=%fused_computation | custom fusion | bytes 4727808 | tf_op jit(solution)/shard_map/gather | solution.py:66
  181.0 20.5 %all-to-all-done = bf16[32,72,739]{2,1,0:T(8,128)(2,1)} async-done(((bf16[32,72,739]{2,1,0:T(8,128)(2,1)}), bf16[32,72,739]{2,1,0:T(8,128)(2,1)}, u32[]{:S(2)}, u32[]{:S(2)}) %all-to-all-start) | async-done | bytes 3405344 | tf_op jit(solution)/shard_map/all_to_all | solution.py:49
  201.5 2.0 convolution_convert_fusion.2
  203.6 3.9 convolution_convert_fusion.1
  208.2 9.1 %multiply_convert_fusion = (bf16[2304,512]{1,0:T(8,128)(2,1)}, bf16[2304,512]{1,0:T(8,128)(2,1)}, bf16[2304,512]{1,0:T(8,128)(2,1)}, bf16[2304,512]{1,0:T(8,128)(2,1)}) fusion(bf16[2304,512]{1,0:T(8,128)(2,1)S(1)} %convolution_convert_fusion.1, bf16[2304,512]{1,0:T(8,128)(2,1)S(1)} %copy-done.6, bf16[2304,512]{1,0:T(8,128)(2,1)S(1)} %copy-done.7, ...), kind=kOutput, calls=%fused_computation.21 | convolution fusion | flops 1255145472 | bytes 21757952 | tf_op jit(solution)/shard_map/dot_general | solution.py:25
  217.3 17.0 %scatter_custom_fusion.1 = f32[1280,512]{1,0:T(8,128)S(1)} fusion(s32[2304]{0:T(1024)S(1)} %get-tuple-element.7, bf16[2304,512]{1,0:T(8,128)(2,1)} %get-tuple-element.14, f32[]{:T(128)} %constant.20.clone.1), kind=kCustom, calls=%fused_computation.17 | custom fusion | flops 2359296 | bytes 4980740 | tf_op jit(solution)/shard_map/scatter-add | solution.py:86
  234.3 17.5 %scatter_custom_fusion.2 = f32[1280,512]{1,0:T(8,128)S(1)} fusion(f32[1280,512]{1,0:T(8,128)S(1)} %scatter_custom_fusion.1, s32[2304]{0:T(1024)S(1)} %get-tuple-element.6, bf16[2304,512]{1,0:T(8,128)(2,1)} %get-tuple-element.12), kind=kCustom, calls=%fused_computation.15 | custom fusion | flops 2359296 | bytes 4980736 | tf_op jit(solution)/shard_map/scatter-add | solution.py:86
  251.9 17.4 %scatter_custom_fusion.3 = f32[1280,512]{1,0:T(8,128)S(1)} fusion(f32[1280,512]{1,0:T(8,128)S(1)} %scatter_custom_fusion.2, s32[2304]{0:T(1024)S(1)} %get-tuple-element.5, bf16[2304,512]{1,0:T(8,128)(2,1)} %get-tuple-element.11), kind=kCustom, calls=%fused_computation.12 | custom fusion | flops 2359296 | bytes 4980736 | tf_op jit(solution)/shard_map/scatter-add | solution.py:86
  269.2 1.5 copy-done.2
  270.8 4.8 fusion.24
  275.6 5.2 fusion.12
  280.8 5.5 fusion.7
  286.6 19.0 %reduce-scatter.2.cloned.1.call-done = f32[320,512]{1,0:T(8,128)} async-done(((f32[1280,512]{1,0:T(8,128)}), f32[320,512]{1,0:T(8,128)}) %reduce-scatter.2.cloned.1.call-update) | async-done | bytes 655376 | tf_op jit(solution)/shard_map/reduce_scatter | solution.py:87
  305.7 2.5 convolution_bitcast_fusion
  308.2 141.0 %all-reduce.3.cloned.1.call-done = (f32[512,512]{1,0:T(8,128)}, f32[512,512]{1,0:T(8,128)}, f32[512,227]{0,1:T(8,128)}) async-done(((f32[512,512]{1,0:T(8,128)}, f32[512,512]{1,0:T(8,128)}, f32[512,227]{0,1:T(8,128)}), (f32[512,512]{1,0:T(8,128)}, f32[512,512]{1,0:T(8,128)}, f32[512,227]{0,1:T(8,128)})) %all-reduce.3.cloned.1.call-update) | async-done | bytes 2562064 | tf_op jit(solution)/shard_map/psum | solution.py:93
  449.2 1.9 broadcast_multiply_fusion.3
  451.1 2.3 broadcast_multiply_fusion.1
  453.4 1.1 broadcast_multiply_fusion
  454.5 1.1 convolution_convert_fusion.3
  455.6 194.9 %all-gather.6.cloned.1.call-done = f32[16384,512]{0,1:T(8,128)} async-done(((f32[512,512]{0,1:T(8,128)}), f32[16384,512]{0,1:T(8,128)}) %all-gather.6.cloned.1.call-update) | async-done | bytes 33554448 | tf_op jit(solution)/shard_map/all_gather | solution.py:94
  650.5 32.5 %copy.20 = f32[64,8,32,512]{3,2,1,0:T(8,128)S(1)} copy(f32[64,8,32,512]{3,1,2,0:T(8,128)} %bitcast.35) | data formatting | bytes 67108864
  683.1 5.4 bitcast_reduce_fusion
  688.8 1.1 broadcast_multiply_fusion.2
  (48 shorter events, 2.6 us)
Async XLA Ops:
  7.2 200.4 %copy-start = (bf16[512,512]{1,0:T(8,128)(2,1)S(1)}, bf16[512,512]{1,0:T(8,128)(2,1)}, u32[]{:S(2)}) copy-start(bf16[512,512]{1,0:T(8,128)(2,1)} %param.16) | copy-start | bytes 1572868
  113.9 7.6 %copy-start.9 = (bf16[512,512]{1,0:T(8,128)(2,1)S(1)}, bf16[512,512]{1,0:T(8,128)(2,1)}, u32[]{:S(2)}) copy-start(bf16[512,512]{1,0:T(8,128)(2,1)} %param.14) | copy-start | bytes 1572868
  113.9 7.6 %copy-start.11 = (bf16[320,512]{1,0:T(8,128)(2,1)S(1)}, bf16[320,512]{1,0:T(8,128)(2,1)}, u32[]{:S(2)}) copy-start(bf16[320,512]{1,0:T(8,128)(2,1)} %param.11) | copy-start | bytes 983044
  113.9 8.7 %copy-start.14 = (s32[3,2304]{1,0:T(4,128)S(1)}, s32[3,2304]{1,0:T(4,128)}, u32[]{:S(2)}) copy-start(s32[3,2304]{1,0:T(4,128)} %param.13) | copy-start | bytes 82948
  114.0 87.6 %all-to-all-start = ((bf16[32,72,739]{2,1,0:T(8,128)(2,1)}), bf16[32,72,739]{2,1,0:T(8,128)(2,1)}, u32[]{:S(2)}, u32[]{:S(2)}) async-start(bf16[32,72,739]{2,1,0:T(8,128)(2,1)} %scatter_fusion), calls=%async_computation | async-start | bytes 7077888 | tf_op jit(solution)/shard_map/all_to_all | solution.py:49
  121.5 35.3 %all-gather.4.cloned.1.call-start = ((), (), s32[]{:S(2)}) async-start(), calls=%async_computation.2 | async-start | bytes 1638400 | tf_op jit(solution)/shard_map/all_gather | solution.py:60
  122.6 183.1 %reduce-scatter.2.cloned.1.call-start = ((), (), s32[]{:S(2)}) async-start(), calls=%async_computation.3 | async-start | bytes 3276800 | tf_op jit(solution)/shard_map/reduce_scatter | solution.py:87
  156.8 9.2 %copy-start.1 = (bf16[1280,512]{1,0:T(8,128)(2,1)S(1)}, bf16[1280,512]{1,0:T(8,128)(2,1)}, u32[]{:S(2)}) copy-start(bf16[1280,512]{1,0:T(8,128)(2,1)} %all-gather.4.cloned.1.call-done) | copy-start | bytes 3932164
  173.5 28.0 %copy-start.13 = (bf16[512,227]{0,1:T(8,128)(2,1)S(1)}, bf16[512,227]{0,1:T(8,128)(2,1)}, u32[]{:S(2)}) copy-start(bf16[512,227]{0,1:T(8,128)(2,1)} %param.17) | copy-start | bytes 697348
  181.0 22.6 %copy-start.15 = (bf16[512,512]{1,0:T(8,128)(2,1)S(1)}, bf16[512,512]{1,0:T(8,128)(2,1)}, u32[]{:S(2)}) copy-start(bf16[512,512]{1,0:T(8,128)(2,1)} %param.15) | copy-start | bytes 1572868
  203.6 4.0 copy-start.5
  203.6 4.0 copy-start.6
  203.6 4.0 copy-start.7
  203.6 4.6 copy-start.8
  269.2 1.5 copy-start.2
  270.8 178.4 %all-reduce.3.cloned.1.call-start = ((), (), s32[]{:S(2)}) async-start(), calls=%async_computation.5 | async-start | bytes 5144576 | tf_op jit(solution)/shard_map/psum | solution.py:93
  275.6 5.2 copy-start.4
  286.4 364.2 %all-gather.6.cloned.1.call-start = ((), (), s32[]{:S(2)}) async-start(), calls=%async_computation.4 | async-start | bytes 34603008 | tf_op jit(solution)/shard_map/all_gather | solution.py:94
  308.2 146.3 %copy-start.3 = (f32[320,512]{1,0:T(8,128)S(1)}, f32[320,512]{1,0:T(8,128)}, u32[]{:S(2)}) copy-start(f32[320,512]{1,0:T(8,128)} %reduce-scatter.2.cloned.1.call-done) | copy-start | bytes 1966084
  308.2 146.3 %copy-start.10 = (bf16[512,512]{1,0:T(8,128)(2,1)S(1)}, bf16[512,512]{1,0:T(8,128)(2,1)}, u32[]{:S(2)}) copy-start(bf16[512,512]{1,0:T(8,128)(2,1)} %param.14) | copy-start | bytes 1572868
  449.2 4.2 copy-start.12
Sparse Core Ops, SparseCore 0:
  124.4 32.3 all-gather.3
  270.9 34.7 reduce-scatter.1
  312.1 137.0 all-reduce.2
  452.6 197.9 all-gather.5
